TPU v7x, 8 devices: a whole 2x2x1 slice. The times are simulated.
8 devices in a mesh: dp: 2 (over z, y), sp: 4 (over x, core).
Axes of the slice: x: 2, y: 2, z: 1, core: 2. Of those that a mesh axis runs over, the one named last changes fastest.
Arguments:
- x_in: bfloat16 [16, 4096, 1152], P('dp', 'sp'), parts along dimension 0
- dy_in: bfloat16 [16, 4096, 1152], P('dp', 'sp'), parts along dimension 0
- positions: int32 [8192], P(('dp', 'sp')), parts along dimension 0
- w_q: bfloat16 [1152, 1024], replicated
- w_k: bfloat16 [1152, 256], replicated
- w_v: bfloat16 [1152, 256], replicated
- w_o: bfloat16 [1024, 1152], replicated
- w_pre: float32 [1152], replicated
- w_post: float32 [1152], replicated
- q_norm: float32 [256], replicated
- k_norm: float32 [256], replicated
Outputs:
- output 1: bfloat16 [16, 4096, 1152], P('dp', 'sp'), parts along dimension 0
- output 2: bfloat16 [16, 4096, 1152], P('dp', 'sp'), parts along dimension 0
- output 3: bfloat16 [2304, 1024], P('dp'), parts along dimension 0
- output 4: bfloat16 [2304, 256], P('dp'), parts along dimension 0
- output 5: bfloat16 [2304, 256], P('dp'), parts along dimension 0
- output 6: bfloat16 [2048, 1152], P('dp'), parts along dimension 0
- output 7: float32 [2304], P('dp'), parts along dimension 0
- output 8: float32 [2304], P('dp'), parts along dimension 0
- output 9: float32 [512], P('dp'), parts along dimension 0
- output 10: float32 [512], P('dp'), parts along dimension 0
There are 2 independent parts. A program takes and returns all parts, laid end to end along the dimension named above; an argument that names none is the same for every part.
All inputs are finite; a program needn't handle non-finite values.
Results may differ from a plain program's by a relative error of at most 0.018656.
Values are sent between devices in bfloat16 or wider.
A program may use at most 1 GiB of HBM per device.

v0:
```python
import functools
import jax
import jax.numpy as jnp
from jax import lax
from jax.sharding import PartitionSpec as P

EPS = 1e-6
ROPE_BASE = 1000000.0
ROPE_SCALE = 8.0
NEG_BIG = -1e30
Q_BLOCK = 1024


def rms_scale(x_f32, weight):
    inv_rms = lax.rsqrt(jnp.mean(x_f32 * x_f32, axis=-1, keepdims=True) + EPS)
    return x_f32 * inv_rms * (1.0 + weight)


def pre_norm(x_f32, weight):
    return rms_scale(x_f32, weight).astype(jnp.bfloat16)


def post_norm(proj, weight):
    return rms_scale(proj.astype(jnp.float32), weight)


def rope_tables(positions, head):
    half_dim = head // 2
    inv_freq = ROPE_BASE ** (-jnp.arange(half_dim, dtype=jnp.float32) * 2.0 / head)
    angles = (positions.astype(jnp.float32) / ROPE_SCALE)[:, None] * inv_freq[None, :]
    return jnp.cos(angles), jnp.sin(angles)


def norm_rope(heads_bf, weight, cosines, sines):
    half_dim = heads_bf.shape[-1] // 2
    normed = rms_scale(heads_bf.astype(jnp.float32), weight)
    first = normed[..., :half_dim]
    second = normed[..., half_dim:]
    cos_b = cosines[None, :, None, :]
    sin_b = sines[None, :, None, :]
    rotated = jnp.concatenate([first * cos_b - second * sin_b, second * cos_b + first * sin_b], axis=-1)
    return rotated.astype(jnp.bfloat16)


def causal_mask(start, block, end):
    row_ids = start + jnp.arange(block)
    col_ids = jnp.arange(end)
    return row_ids[:, None] >= col_ids[None, :]


def attention_fwd(q_all, k_all, v_all):
    batch, seq, q_heads, head = q_all.shape
    kv_loc = k_all.shape[2]
    scale = head ** -0.5
    block = min(Q_BLOCK, seq)
    q_grp = q_all.reshape(batch, seq, kv_loc, q_heads // kv_loc, head)
    pieces = []
    row_lse = []
    for index in range(seq // block):
        start = index * block
        end = start + block
        scores = jnp.einsum('bqkgh,bskh->bkgqs', q_grp[:, start:end], k_all[:, :end], preferred_element_type=jnp.float32) * scale
        scores = jnp.where(causal_mask(start, block, end), scores, NEG_BIG)
        row_max = jnp.max(scores, axis=-1, keepdims=True)
        exp_scores = jnp.exp(scores - row_max)
        row_sum = jnp.sum(exp_scores, axis=-1, keepdims=True)
        attn_prob = (exp_scores / row_sum).astype(jnp.bfloat16)
        pieces.append(jnp.einsum('bkgqs,bskh->bqkgh', attn_prob, v_all[:, :end], preferred_element_type=jnp.float32).astype(jnp.bfloat16))
        row_lse.append(row_max + jnp.log(row_sum))
    return jnp.concatenate(pieces, axis=1).reshape(batch, seq, q_heads, head), row_lse


def attention_bwd(q_all, k_all, v_all, row_lse, d_out):
    batch, seq, q_heads, head = q_all.shape
    kv_loc = k_all.shape[2]
    per_kv = q_heads // kv_loc
    scale = head ** -0.5
    block = min(Q_BLOCK, seq)
    q_grp = q_all.reshape(batch, seq, kv_loc, per_kv, head)
    do_grp = d_out.reshape(batch, seq, kv_loc, per_kv, head)
    dk_acc = jnp.zeros(k_all.shape, jnp.float32)
    dv_acc = jnp.zeros(v_all.shape, jnp.float32)
    dq_pieces = []
    for index in range(seq // block):
        start = index * block
        end = start + block
        q_blk = q_grp[:, start:end]
        do_blk = do_grp[:, start:end]
        k_pre = k_all[:, :end]
        v_pre = v_all[:, :end]
        scores = jnp.einsum('bqkgh,bskh->bkgqs', q_blk, k_pre, preferred_element_type=jnp.float32) * scale
        scores = jnp.where(causal_mask(start, block, end), scores, NEG_BIG)
        attn_prob = jnp.exp(scores - row_lse[index])
        d_prob = jnp.einsum('bqkgh,bskh->bkgqs', do_blk, v_pre, preferred_element_type=jnp.float32)
        d_score = (attn_prob * (d_prob - jnp.sum(d_prob * attn_prob, axis=-1, keepdims=True)) * scale).astype(jnp.bfloat16)
        dq_pieces.append(jnp.einsum('bkgqs,bskh->bqkgh', d_score, k_pre, preferred_element_type=jnp.float32).astype(jnp.bfloat16))
        dk_part = jnp.einsum('bkgqs,bqkgh->bskh', d_score, q_blk, preferred_element_type=jnp.float32)
        dv_part = jnp.einsum('bkgqs,bqkgh->bskh', attn_prob.astype(jnp.bfloat16), do_blk, preferred_element_type=jnp.float32)
        dk_acc = lax.dynamic_update_slice(dk_acc, dk_acc[:, :end] + dk_part, (0, 0, 0, 0))
        dv_acc = lax.dynamic_update_slice(dv_acc, dv_acc[:, :end] + dv_part, (0, 0, 0, 0))
    dq_all = jnp.concatenate(dq_pieces, axis=1).reshape(batch, seq, q_heads, head)
    return dq_all, dk_acc.astype(jnp.bfloat16), dv_acc.astype(jnp.bfloat16)


def fold_copies(grad_wide, kv_heads, rep):
    if rep == 1:
        return grad_wide
    batch, seq_loc, wide, head = grad_wide.shape
    summed = jnp.sum(grad_wide.reshape(batch, seq_loc, kv_heads, rep, head), axis=3, dtype=jnp.float32)
    return summed.astype(jnp.bfloat16)


def solution(mesh):
    group = mesh.shape['sp']

    def to_heads(arr):
        return lax.all_to_all(arr, 'sp', 2, 1, tiled=True)

    def to_tokens(arr):
        return lax.all_to_all(arr, 'sp', 1, 2, tiled=True)

    def device_step(x_in, dy_in, positions, w_q, w_k, w_v, w_o, w_pre, w_post, q_norm, k_norm):
        batch, seq_loc, width = x_in.shape
        head = q_norm.shape[0]
        heads = w_q.shape[1] // head
        kv_heads = w_k.shape[1] // head
        rep = max(1, group // kv_heads)
        x_f32 = x_in.astype(jnp.float32)
        normed, pre_pull = jax.vjp(pre_norm, x_f32, w_pre)
        q_proj = jnp.einsum('bsd,dn->bsn', normed, w_q, preferred_element_type=jnp.float32).astype(jnp.bfloat16).reshape(batch, seq_loc, heads, head)
        k_proj = jnp.einsum('bsd,dn->bsn', normed, w_k, preferred_element_type=jnp.float32).astype(jnp.bfloat16).reshape(batch, seq_loc, kv_heads, head)
        v_proj = jnp.einsum('bsd,dn->bsn', normed, w_v, preferred_element_type=jnp.float32).astype(jnp.bfloat16).reshape(batch, seq_loc, kv_heads, head)
        cosines, sines = rope_tables(positions, head)
        q_rot, q_pull = jax.vjp(functools.partial(norm_rope, cosines=cosines, sines=sines), q_proj, q_norm)
        k_rot, k_pull = jax.vjp(functools.partial(norm_rope, cosines=cosines, sines=sines), k_proj, k_norm)
        q_all = to_heads(q_rot)
        k_all = to_heads(jnp.repeat(k_rot, rep, axis=2))
        v_all = to_heads(jnp.repeat(v_proj, rep, axis=2))
        o_all, row_lse = attention_fwd(q_all, k_all, v_all)
        o_flat = to_tokens(o_all).reshape(batch, seq_loc, heads * head)
        proj = jnp.einsum('bsn,nd->bsd', o_flat, w_o, preferred_element_type=jnp.float32).astype(jnp.bfloat16)
        post, post_pull = jax.vjp(post_norm, proj, w_post)
        y_out = (x_f32 + post).astype(jnp.bfloat16)
        dy_f32 = dy_in.astype(jnp.float32)
        d_proj, dw_post = post_pull(dy_f32)
        dw_o = jnp.einsum('bsn,bsd->nd', o_flat, d_proj, preferred_element_type=jnp.float32)
        d_oflat = jnp.einsum('bsd,nd->bsn', d_proj, w_o, preferred_element_type=jnp.float32).astype(jnp.bfloat16)
        d_oall = to_heads(d_oflat.reshape(batch, seq_loc, heads, head))
        dq_all, dk_all, dv_all = attention_bwd(q_all, k_all, v_all, row_lse, d_oall)
        dq_rot = to_tokens(dq_all)
        dk_rot = fold_copies(to_tokens(dk_all), kv_heads, rep)
        dv_proj = fold_copies(to_tokens(dv_all), kv_heads, rep)
        dq_proj, dq_norm = q_pull(dq_rot)
        dk_proj, dk_norm = k_pull(dk_rot)
        dq_flat = dq_proj.reshape(batch, seq_loc, heads * head)
        dk_flat = dk_proj.reshape(batch, seq_loc, kv_heads * head)
        dv_flat = dv_proj.reshape(batch, seq_loc, kv_heads * head)
        dw_q = jnp.einsum('bsd,bsn->dn', normed, dq_flat, preferred_element_type=jnp.float32)
        dw_k = jnp.einsum('bsd,bsn->dn', normed, dk_flat, preferred_element_type=jnp.float32)
        dw_v = jnp.einsum('bsd,bsn->dn', normed, dv_flat, preferred_element_type=jnp.float32)
        d_normed = (jnp.einsum('bsn,dn->bsd', dq_flat, w_q, preferred_element_type=jnp.float32)
                    + jnp.einsum('bsn,dn->bsd', dk_flat, w_k, preferred_element_type=jnp.float32)
                    + jnp.einsum('bsn,dn->bsd', dv_flat, w_v, preferred_element_type=jnp.float32)).astype(jnp.bfloat16)
        dx_norm, dw_pre = pre_pull(d_normed)
        dx_out = (dy_f32 + dx_norm).astype(jnp.bfloat16)
        sums = lax.psum((dw_q, dw_k, dw_v, dw_o, dw_pre, dw_post, dq_norm, dk_norm), 'sp')
        return (y_out, dx_out, sums[0].astype(jnp.bfloat16), sums[1].astype(jnp.bfloat16), sums[2].astype(jnp.bfloat16), sums[3].astype(jnp.bfloat16), sums[4], sums[5], sums[6], sums[7])

    token_spec = P('dp', 'sp', None)
    return jax.shard_map(device_step, mesh=mesh,
                         in_specs=(token_spec, token_spec, P(('dp', 'sp')), P(None, None), P(None, None), P(None, None), P(None, None), P(None), P(None), P(None), P(None)),
                         out_specs=(token_spec, token_spec, P('dp', None), P('dp', None), P('dp', None), P('dp', None), P('dp'), P('dp'), P('dp'), P('dp')),
                         check_vma=False)
```

profile of v0, /device:TPU:0, one launch (start us, length us, event | category | flops | bytes accessed | tf_op | source)
XLA Modules:
  0.0 3343.5 jit_solution(2339748049955813734)
XLA Ops:
  74.8 166.0 %all-to-all-done.1 = bf16[8,1024,4,256]{3,1,0,2:T(8,128)(2,1)} async-done(((bf16[8,1024,4,256]{3,1,0,2:T(8,128)(2,1)}), bf16[8,1024,4,256]{3,1,0,2:T(8,128)(2,1)}, u32[]{:S(2)}, u32[]{:S(2)}) %all-to-all-start.1) | async-done | bytes 16777248 | tf_op jit(solution)/shard_map/all_to_all | solution.py:117
  373.6 64.5 %all-to-all-done = bf16[8,1024,4,256]{1,3,0,2:T(8,128)(2,1)} async-done(((bf16[8,1024,4,256]{1,3,0,2:T(8,128)(2,1)}), bf16[8,1024,4,256]{1,3,0,2:T(8,128)(2,1)}, u32[]{:S(2)}, u32[]{:S(2)}) %all-to-all-start) | async-done | bytes 16777248 | tf_op jit(solution)/shard_map/all_to_all | solution.py:117
  544.8 91.2 %all-to-all-done.2 = bf16[8,1024,4,256]{1,3,0,2:T(8,128)(2,1)} async-done(((bf16[8,1024,4,256]{1,3,0,2:T(8,128)(2,1)}), bf16[8,1024,4,256]{1,3,0,2:T(8,128)(2,1)}, u32[]{:S(2)}, u32[]{:S(2)}) %all-to-all-start.2) | async-done | bytes 16777248 | tf_op jit(solution)/shard_map/all_to_all | solution.py:117
  783.0 41.5 %fusion.140 = (f32[8,1024]{1,0:T(8,128)S(1)}, f32[8,1,1,1024,3072]{3,4,0,2,1:T(8,128)}) fusion(bf16[8,4096,1,1,256]{4,1,0,3,2:T(8,128)(2,1)} %bitcast.504, bf16[8,4096,1,256]{3,1,0,2:T(8,128)(2,1)} %bitcast.480, pred[1024,3072]{0,1:T(8,128)(4,1)} %iota_compare_fusion.1), kind=kOutput, calls=%fused_computation.243 | convolution fusion | flops 12960391168 | bytes 120619008 | tf_op jit(solution)/shard_map/bqkgh,bskh->bkgqs/dot_general | solution.py:62
  855.5 40.0 %convert_bitcast_fusion.7 = bf16[8,1024,1,1,256]{1,4,0,3,2:T(8,128)(2,1)} fusion(f32[8,1024]{1,0:T(8,128)S(1)} %fusion.10, f32[8,1,1,1024,3072]{3,4,0,2,1:T(8,128)} %get-tuple-element.44, f32[8,1024]{1,0:T(8,128)S(1)} %get-tuple-element.43, bf16[8,4096,1,256]{1,3,0,2:T(8,128)(2,1)} %bitcast.496), kind=kOutput, calls=%fused_computation.188 | convolution fusion | flops 12962496512 | bytes 117506048 | tf_op jit(solution)/shard_map/bkgqs,bskh->bqkgh/dot_general | solution.py:68
  895.5 54.7 %fusion.139 = (f32[8,1024]{1,0:T(8,128)S(1)}, f32[8,1,1,1024,4096]{3,4,0,2,1:T(8,128)}) fusion(bf16[8,4096,256]{2,1,0:T(8,128)(2,1)} %bitcast.481, bf16[8,4096,1,1,256]{4,1,0,3,2:T(8,128)(2,1)} %bitcast.505, pred[1024,4096]{0,1:T(8,128)(4,1)} %iota_compare_fusion), kind=kOutput, calls=%fused_computation.242 | convolution fusion | flops 17280524288 | bytes 159416320 | tf_op jit(solution)/shard_map/bqkgh,bskh->bkgqs/dot_general | solution.py:62
  950.2 40.8 %fusion.4 = f32[8,1024]{1,0:T(8,128)S(1)} fusion(f32[8,1,1,1024,4096]{3,4,0,2,1:T(8,128)} %get-tuple-element.42, f32[8,1024]{1,0:T(8,128)S(1)} %get-tuple-element.41), kind=kLoop, calls=%fused_computation.10 | loop fusion | flops 67100672 | bytes 134283264 | tf_op jit(solution)/shard_map/reduce_sum | solution.py:66
  991.1 49.8 %convert_bitcast_fusion.6 = bf16[8,1024,1,1,256]{1,4,0,3,2:T(8,128)(2,1)} fusion(bf16[8,4096,256]{1,2,0:T(8,128)(2,1)} %reshape.530, f32[8,1024]{1,0:T(8,128)S(1)} %fusion.4, f32[8,1,1,1024,4096]{3,4,0,2,1:T(8,128)} %get-tuple-element.42, f32[8,1024]{1,0:T(8,128)S(1)} %get-tuple-element.41), kind=kOutput, calls=%fused_computation.187 | convolution fusion | flops 17282629632 | bytes 155254784 | tf_op jit(solution)/shard_map/bkgqs,bskh->bqkgh/dot_general | solution.py:68
  1085.4 182.7 %all-to-all-done.3 = bf16[8,4096,1,256]{3,0,2,1:T(8,128)(2,1)} async-done(((bf16[8,4096,1,256]{3,0,2,1:T(8,128)(2,1)}), bf16[8,4096,1,256]{3,0,2,1:T(8,128)(2,1)}, u32[]{:S(2)}, u32[]{:S(2)}) %all-to-all-start.3) | async-done | bytes 16777248 | tf_op jit(solution)/shard_map/all_to_all | solution.py:120
  1430.1 181.9 %all-to-all-done.4 = bf16[8,1024,4,256]{1,3,0,2:T(8,128)(2,1)} async-done(((bf16[8,1024,4,256]{1,3,0,2:T(8,128)(2,1)}), bf16[8,1024,4,256]{1,3,0,2:T(8,128)(2,1)}, u32[]{:S(2)}, u32[]{:S(2)}) %all-to-all-start.4) | async-done | bytes 16777248 | tf_op jit(solution)/shard_map/all_to_all | solution.py:117
  1678.1 49.0 %fusion.16 = (f32[8,1024]{1,0:T(8,128)}, f32[8,2048,1024]{2,1,0:T(8,128)}) fusion(f32[8,1,1,1024,2048]{3,4,0,2,1:T(8,128)} %get-tuple-element.46, f32[8,1024]{1,0:T(8,128)S(1)} %log_add_fusion.2, bf16[8,4096,1,1,256]{4,1,0,3,2:T(8,128)(2,1)} %bitcast.488, bf16[8,4096,1,256]{1,3,0,2:T(8,128)(2,1)} %bitcast.498), kind=kOutput, calls=%fused_computation.35 | convolution fusion | flops 8640258048 | bytes 146866176 | tf_op jit(solution)/shard_map/bqkgh,bskh->bkgqs/dot_general | solution.py:94
  1740.9 34.7 %fusion.68 = f32[8,4096,1,256]{1,3,0,2:T(8,128)} fusion(f32[8,4096,1,256]{1,3,0,2:T(8,128)} %dynamic_update_slice.21, f32[8,1,1,1024,2048]{3,4,0,2,1:T(8,128)} %get-tuple-element.46, f32[8,1024]{1,0:T(8,128)S(1)} %log_add_fusion.2, bf16[8,4096,1,1,256]{4,1,0,3,2:T(8,128)(2,1)} %bitcast.489), kind=kOutput, calls=%fused_computation.121 | convolution fusion | flops 8627683328 | bytes 104890368 | tf_op jit(solution)/shard_map/bkgqs,bqkgh->bskh/dot_general | solution.py:98
  1775.7 70.1 %fusion.6 = (f32[8,1024]{1,0:T(8,128)}, f32[8,3072,1024]{2,1,0:T(8,128)}) fusion(f32[8,1,1,1024,3072]{3,4,0,2,1:T(8,128)} %get-tuple-element.44, f32[8,1024]{1,0:T(8,128)S(1)} %log_add_fusion.1, bf16[8,4096,1,1,256]{4,1,0,3,2:T(8,128)(2,1)} %bitcast.490, bf16[8,4096,1,256]{1,3,0,2:T(8,128)(2,1)} %bitcast.499), kind=kOutput, calls=%fused_computation.15 | convolution fusion | flops 12960391168 | bytes 218169344 | tf_op jit(solution)/shard_map/bqkgh,bskh->bkgqs/dot_general | solution.py:94
  1845.8 50.6 %fusion.62 = f32[8,4096,1,256]{1,3,0,2:T(8,128)} fusion(f32[8,4096,1,256]{1,3,0,2:T(8,128)} %fusion.68, f32[8,1,1,1024,3072]{3,4,0,2,1:T(8,128)} %get-tuple-element.44, f32[8,1024]{1,0:T(8,128)S(1)} %log_add_fusion.1, bf16[8,4096,1,1,256]{4,1,0,3,2:T(8,128)(2,1)} %bitcast.491), kind=kOutput, calls=%fused_computation.110 | convolution fusion | flops 12941524992 | bytes 155222016 | tf_op jit(solution)/shard_map/bkgqs,bqkgh->bskh/dot_general | solution.py:98
  1896.4 93.7 %fusion = (f32[8,1024]{1,0:T(8,128)}, f32[8,4096,1024]{2,1,0:T(8,128)}) fusion(f32[8,1,1,1024,4096]{3,4,0,2,1:T(8,128)} %get-tuple-element.42, f32[8,1024]{1,0:T(8,128)S(1)} %copy-done.18, bf16[8,4096,256]{1,2,0:T(8,128)(2,1)} %reshape.530, bf16[8,4096,1,1,256]{4,1,0,3,2:T(8,128)(2,1)} %bitcast.492), kind=kOutput, calls=%fused_computation.3 | convolution fusion | flops 17280524288 | bytes 289472512 | tf_op jit(solution)/shard_map/bqkgh,bskh->bkgqs/dot_general | solution.py:94
  1990.1 59.3 %fusion.51 = bf16[8,4096,1,256]{1,3,0,2:T(8,128)(2,1)} fusion(f32[8,4096,1,256]{1,3,0,2:T(8,128)} %fusion.62, f32[8,1,1,1024,4096]{3,4,0,2,1:T(8,128)} %get-tuple-element.42, f32[8,1024]{1,0:T(8,128)S(1)} %copy-done.18, bf16[8,4096,1,1,256]{4,1,0,3,2:T(8,128)(2,1)} %bitcast.493), kind=kOutput, calls=%fused_computation.85 | convolution fusion | flops 17263755264 | bytes 188776448 | tf_op jit(solution)/shard_map/bkgqs,bqkgh->bskh/dot_general | solution.py:98
  2133.4 53.6 %fusion.50 = bf16[8,1024,2048]{1,2,0:T(8,128)(2,1)} fusion(f32[8,2048,1024]{2,1,0:T(8,128)} %get-tuple-element.54, f32[8,1,1,1024,2048]{3,4,0,2,1:T(8,128)} %get-tuple-element.46, f32[8,1024]{1,0:T(8,128)S(1)} %copy-done.39, f32[8,1024]{1,0:T(8,128)S(1)} %copy-done.7), kind=kLoop, calls=%fused_computation.83 | loop fusion | flops 83886080 | bytes 167837696 | tf_op jit(solution)/shard_map/reshape.94
  2211.2 79.1 %fusion.28 = bf16[8,1024,3072]{1,2,0:T(8,128)(2,1)} fusion(f32[8,3072,1024]{2,1,0:T(8,128)} %get-tuple-element.56, f32[8,1,1,1024,3072]{3,4,0,2,1:T(8,128)} %get-tuple-element.44, f32[8,1024]{1,0:T(8,128)S(1)} %copy-done.38, f32[8,1024]{1,0:T(8,128)S(1)} %copy-done.5), kind=kLoop, calls=%fused_computation.58 | loop fusion | flops 125829120 | bytes 251723776 | tf_op jit(solution)/shard_map/reshape.102
  2290.2 104.4 %fusion.15 = bf16[8,1024,4096]{1,2,0:T(8,128)(2,1)} fusion(f32[8,4096,1024]{2,1,0:T(8,128)} %get-tuple-element.58, f32[8,1,1,1024,4096]{3,4,0,2,1:T(8,128)} %get-tuple-element.42, f32[8,1024]{1,0:T(8,128)S(1)} %copy-done.59, f32[8,1024]{1,0:T(8,128)S(1)} %copy-done.19), kind=kLoop, calls=%fused_computation.31 | loop fusion | flops 167772160 | bytes 335609856 | tf_op jit(solution)/shard_map/reshape.110
  2394.6 36.0 %fusion.63 = f32[8,4096,1,256]{1,3,0,2:T(8,128)} fusion(f32[8,4096,1,256]{1,3,0,2:T(8,128)} %fusion.69, bf16[8,1024,3072]{1,2,0:T(8,128)(2,1)} %fusion.28, bf16[8,4096,1,1,256]{4,1,0,3,2:T(8,128)(2,1)} %bitcast.508), kind=kOutput, calls=%fused_computation.112 | convolution fusion | flops 12891193344 | bytes 104857600 | tf_op jit(solution)/shard_map/bkgqs,bqkgh->bskh/dot_general | solution.py:97
  2430.6 40.1 %fusion.52 = bf16[8,4096,1,256]{1,3,0,2:T(8,128)(2,1)} fusion(f32[8,4096,1,256]{1,3,0,2:T(8,128)} %fusion.63, bf16[8,1024,4096]{1,2,0:T(8,128)(2,1)} %fusion.15, bf16[8,4096,1,1,256]{4,1,0,3,2:T(8,128)(2,1)} %bitcast.509), kind=kOutput, calls=%fused_computation.87 | convolution fusion | flops 17196646400 | bytes 121634816 | tf_op jit(solution)/shard_map/bkgqs,bqkgh->bskh/dot_general | solution.py:97
  2627.3 100.9 %all-to-all-done.6 = bf16[8,4096,1,256]{3,0,2,1:T(8,128)(2,1)} async-done(((bf16[8,4096,1,256]{3,0,2,1:T(8,128)(2,1)}), bf16[8,4096,1,256]{3,0,2,1:T(8,128)(2,1)}, u32[]{:S(2)}, u32[]{:S(2)}) %all-to-all-start.6) | async-done | bytes 16777248 | tf_op jit(solution)/shard_map/all_to_all | solution.py:120
  3062.4 48.2 %fusion.37 = (f32[1152]{0:T(1024)}, f32[8,1024]{1,0:T(8,128)S(1)}, bf16[8,1024,1152]{2,1,0:T(8,128)(2,1)}) fusion(bf16[8,1024,1152]{2,1,0:T(8,128)(2,1)} %param.11, f32[8,1024]{1,0:T(8,128)S(1)} %copy-done.46, f32[1152]{0:T(1024)S(1)} %copy-done.62, f32[8,1024,1152]{2,1,0:T(8,128)} %fusion.124, f32[8,1024,1152]{2,1,0:T(8,128)} %fusion.95, ...), kind=kOutput, calls=%fused_computation.70 | convolution fusion | flops 19431151616 | bytes 132457472 | tf_op jit(solution)/shard_map/bsn,dn->bsd/dot_general | solution.py:161
  3139.6 203.5 %all-reduce.8 = (bf16[1152,1024]{1,0:T(8,128)(2,1)}, bf16[1152,256]{1,0:T(8,128)(2,1)}, bf16[1152,256]{1,0:T(8,128)(2,1)}, bf16[1024,1152]{1,0:T(8,128)(2,1)}, f...) all-reduce(f32[1152,1024]{1,0:T(8,128)} %convolution_bitcast_fusion, ...), channel_id=1, replica_groups=mesh['dp'=2,'sp'=4] {'sp'}, use_global_device_ids=true, to_apply=%region_22.23 | all-reduce | flops 2951936 | bytes 17717248 | tf_op jit(solution)/shard_map/psum | solution.py:166
  (257 shorter events, 1405.2 us)
Async XLA Ops:
  0.6 256.0 %copy-start = (bf16[1152,1024]{1,0:T(8,128)(2,1)S(1)}, bf16[1152,1024]{1,0:T(8,128)(2,1)}, u32[]{:S(2)}) copy-start(bf16[1152,1024]{1,0:T(8,128)(2,1)} %param.14) | copy-start | bytes 7077892
  2.9 253.7 %copy-start.61 = (f32[1152]{0:T(1024)}, f32[1152]{0:T(1024)S(1)}, u32[]{:S(2)}) copy-start(f32[1152]{0:T(1024)S(1)} %broadcast_add_fusion.1) | copy-start | bytes 13828
  17.4 239.2 %copy-start.45 = (f32[8,1024]{1,0:T(8,128)}, f32[8,1024]{1,0:T(8,128)S(1)}, u32[]{:S(2)}) copy-start(f32[8,1024]{1,0:T(8,128)S(1)} %fusion.128) | copy-start | bytes 98308
  49.6 191.1 %all-to-all-start.1 = ((bf16[8,1024,4,256]{3,1,0,2:T(8,128)(2,1)}), bf16[8,1024,4,256]{3,1,0,2:T(8,128)(2,1)}, u32[]{:S(2)}, u32[]{:S(2)}) async-start(bf16[8,1024,4,256]{3,1,0,2:T(8,128)(2,1)} %reshape.517), calls=%async_computation.1 | async-start | bytes 33554432 | tf_op jit(solution)/shard_map/all_to_all | solution.py:117
  248.2 189.9 %all-to-all-start = ((bf16[8,1024,4,256]{1,3,0,2:T(8,128)(2,1)}), bf16[8,1024,4,256]{1,3,0,2:T(8,128)(2,1)}, u32[]{:S(2)}, u32[]{:S(2)}) async-start(bf16[8,1024,4,256]{1,3,0,2:T(8,128)(2,1)} %reshape.515), calls=%async_computation | async-start | bytes 33554432 | tf_op jit(solution)/shard_map/all_to_all | solution.py:117
  256.6 76.0 %copy-start.16 = (f32[1024,128]{1,0:T(8,128)}, f32[1024,128]{1,0:T(8,128)S(1)}, u32[]{:S(2)}) copy-start(f32[1024,128]{1,0:T(8,128)S(1)} %copy.203) | copy-start | bytes 1572868
  438.1 197.9 %all-to-all-start.2 = ((bf16[8,1024,4,256]{1,3,0,2:T(8,128)(2,1)}), bf16[8,1024,4,256]{1,3,0,2:T(8,128)(2,1)}, u32[]{:S(2)}, u32[]{:S(2)}) async-start(bf16[8,1024,4,256]{1,3,0,2:T(8,128)(2,1)} %copy.204), calls=%async_computation.2 | async-start | bytes 33554432 | tf_op jit(solution)/shard_map/all_to_all | solution.py:117
  703.0 51.5 %copy-start.34 = (f32[8,1024]{1,0:T(8,128)}, f32[8,1024]{1,0:T(8,128)S(1)}, u32[]{:S(2)}) copy-start(f32[8,1024]{1,0:T(8,128)S(1)} %get-tuple-element.45) | copy-start | bytes 98308
  991.1 49.8 %copy-start.57 = (f32[8,1024]{1,0:T(8,128)}, f32[8,1024]{1,0:T(8,128)S(1)}, u32[]{:S(2)}) copy-start(f32[8,1024]{1,0:T(8,128)S(1)} %fusion.4) | copy-start | bytes 98308
  1077.9 190.1 %all-to-all-start.3 = ((bf16[8,4096,1,256]{3,0,2,1:T(8,128)(2,1)}), bf16[8,4096,1,256]{3,0,2,1:T(8,128)(2,1)}, u32[]{:S(2)}, u32[]{:S(2)}) async-start(bf16[8,4096,1,256]{3,0,2,1:T(8,128)(2,1)} %copy.212), calls=%async_computation.3 | async-start | bytes 33554432 | tf_op jit(solution)/shard_map/all_to_all | solution.py:120
  1085.3 292.6 %copy-start.63 = (f32[1152]{0:T(1024)}, f32[1152]{0:T(1024)S(1)}, u32[]{:S(2)}) copy-start(f32[1152]{0:T(1024)S(1)} %broadcast_add_fusion) | copy-start | bytes 13828
  1422.1 189.8 %all-to-all-start.4 = ((bf16[8,1024,4,256]{1,3,0,2:T(8,128)(2,1)}), bf16[8,1024,4,256]{1,3,0,2:T(8,128)(2,1)}, u32[]{:S(2)}, u32[]{:S(2)}) async-start(bf16[8,1024,4,256]{1,3,0,2:T(8,128)(2,1)} %copy.214), calls=%async_computation.4 | async-start | bytes 33554432 | tf_op jit(solution)/shard_map/all_to_all | solution.py:117
  1429.3 223.0 %copy-start.22 = (f32[8,1024]{1,0:T(8,128)}, f32[8,1024]{1,0:T(8,128)S(1)}, u32[]{:S(2)}) copy-start(f32[8,1024]{1,0:T(8,128)S(1)} %log_add_fusion.3) | copy-start | bytes 98308
  1429.4 311.6 %copy-start.6 = (f32[8,1024]{1,0:T(8,128)}, f32[8,1024]{1,0:T(8,128)S(1)}, u32[]{:S(2)}) copy-start(f32[8,1024]{1,0:T(8,128)S(1)} %log_add_fusion.2) | copy-start | bytes 98308
  1429.4 416.3 %copy-start.4 = (f32[8,1024]{1,0:T(8,128)}, f32[8,1024]{1,0:T(8,128)S(1)}, u32[]{:S(2)}) copy-start(f32[8,1024]{1,0:T(8,128)S(1)} %log_add_fusion.1) | copy-start | bytes 98308
  1845.8 50.6 %copy-start.18 = (f32[8,1024]{1,0:T(8,128)S(1)}, f32[8,1024]{1,0:T(8,128)}, u32[]{:S(2)}) copy-start(f32[8,1024]{1,0:T(8,128)} %log_add_fusion) | copy-start | bytes 98308
  2071.9 466.2 %all-to-all-start.7 = ((bf16[8,4096,1,256]{3,0,2,1:T(8,128)(2,1)}), bf16[8,4096,1,256]{3,0,2,1:T(8,128)(2,1)}, u32[]{:S(2)}, u32[]{:S(2)}) async-start(bf16[8,4096,1,256]{3,0,2,1:T(8,128)(2,1)} %copy.253), calls=%async_computation.7 | async-start | bytes 33554432 | tf_op jit(solution)/shard_map/all_to_all | solution.py:120
  2211.1 79.1 %copy-start.19 = (f32[8,1024]{1,0:T(8,128)S(1)}, f32[8,1024]{1,0:T(8,128)}, u32[]{:S(2)}) copy-start(f32[8,1024]{1,0:T(8,128)} %log_add_fusion) | copy-start | bytes 98308
  2211.1 79.1 %copy-start.59 = (f32[8,1024]{1,0:T(8,128)S(1)}, f32[8,1024]{1,0:T(8,128)}, u32[]{:S(2)}) copy-start(f32[8,1024]{1,0:T(8,128)} %get-tuple-element.57) | copy-start | bytes 98308
  2538.1 190.0 %all-to-all-start.6 = ((bf16[8,4096,1,256]{3,0,2,1:T(8,128)(2,1)}), bf16[8,4096,1,256]{3,0,2,1:T(8,128)(2,1)}, u32[]{:S(2)}, u32[]{:S(2)}) async-start(bf16[8,4096,1,256]{3,0,2,1:T(8,128)(2,1)} %copy.242), calls=%async_computation.6 | async-start | bytes 33554432 | tf_op jit(solution)/shard_map/all_to_all | solution.py:120
  2627.3 108.3 %copy-start.48 = (f32[8,1024]{1,0:T(8,128)S(1)}, f32[8,1024]{1,0:T(8,128)}, u32[]{:S(2)}) copy-start(f32[8,1024]{1,0:T(8,128)} %copy-done.47) | copy-start | bytes 98308
  2627.3 108.3 %copy-start.64 = (f32[1152]{0:T(1024)S(1)}, f32[1152]{0:T(1024)}, u32[]{:S(2)}) copy-start(f32[1152]{0:T(1024)} %copy-done.63) | copy-start | bytes 13828
  2627.3 108.3 %copy-start.66 = (f32[8,1024]{1,0:T(8,128)S(1)}, f32[8,1024]{1,0:T(8,128)}, u32[]{:S(2)}) copy-start(f32[8,1024]{1,0:T(8,128)} %copy-done.65) | copy-start | bytes 98308
  2728.1 190.2 %all-to-all-start.5 = ((bf16[8,4096,1,256]{3,0,2,1:T(8,128)(2,1)}), bf16[8,4096,1,256]{3,0,2,1:T(8,128)(2,1)}, u32[]{:S(2)}, u32[]{:S(2)}) async-start(bf16[8,4096,1,256]{3,0,2,1:T(8,128)(2,1)} %copy.228), calls=%async_computation.5 | async-start | bytes 33554432 | tf_op jit(solution)/shard_map/all_to_all | solution.py:120
  (57 other events, 985.9 us)
where the time goes:
time: 3360 us; the launch traced here: 3340 us
  matrix products  1160 us (35%)
  waiting for transfers between devices  820 us (24%)
  other arithmetic  668 us (20%)
  local copies, waits for them, and re-layouts  424 us (13%)
  blocking collectives  203 us (6%)
  starting transfers between devices  66.9 us (2%)
    all_to_all x4, waiting for transfers between devices, to_heads(): return lax.all_to_all(arr, 'sp', 2, 1, tiled=True)  504 us
    all_to_all x4, waiting for transfers between devices, to_tokens(): return lax.all_to_all(arr, 'sp', 1, 2, tiled=True)  317 us
    another operation x5, other arithmetic  277 us
    dot_general x4, matrix products, attention_bwd(): jnp.einsum('bqkgh,bskh->bkgqs', do_blk, v_pre, preferred_element_type=jnp...  239 us
    psum x1, blocking collectives, device_step(): lax.psum((dw_q, dw_k, dw_v, dw_o, dw_pre, dw_post, dq_norm, dk_norm), 'sp')  203 us
    dot_general x4, matrix products, attention_bwd(): jnp.einsum('bkgqs,bqkgh->bskh', attn_prob.astype(jnp.bfloat16), do_blk, p...  163 us
    dot_general x4, matrix products, attention_fwd(): jnp.einsum('bqkgh,bskh->bkgqs', q_grp[:, start:end], k_all[:, :end], pref...  141 us
    dot_general x4, matrix products, attention_fwd(): jnp.einsum('bkgqs,bskh->bqkgh', attn_prob, v_all[:, :end], preferred_elem...  136 us
  transfers between devices with their start and end apart: 8, of which 7 were waited for; matrix products, arithmetic and copies ran while one was open for 27% of the time, Pallas kernels for 0%

commit v1 on v0

v1 whole, which is shorter than its diff:
```python
import functools
import jax
import jax.numpy as jnp
from jax import lax
from jax.experimental import pallas as pl
from jax.experimental.pallas import tpu as pltpu
from jax.sharding import PartitionSpec as P

EPS = 1e-6
ROPE_BASE = 1000000.0
ROPE_SCALE = 8.0
NEG_BIG = -1e30
BLOCK = 512
PAIR = 2
LOG2E = 1.4426950408889634
NT = (((1,), (1,)), ((), ()))
F32 = jnp.float32
BF16 = jnp.bfloat16


def rms_scale(x_f32, weight):
    inv_rms = lax.rsqrt(jnp.mean(x_f32 * x_f32, axis=-1, keepdims=True) + EPS)
    return x_f32 * inv_rms * (1.0 + weight)


def pre_norm(x_f32, weight):
    return rms_scale(x_f32, weight).astype(BF16)


def post_norm(proj, weight):
    return rms_scale(proj.astype(F32), weight)


def rope_tables(positions, head):
    half_dim = head // 2
    inv_freq = ROPE_BASE ** (-jnp.arange(half_dim, dtype=F32) * 2.0 / head)
    angles = (positions.astype(F32) / ROPE_SCALE)[:, None] * inv_freq[None, :]
    return jnp.cos(angles), jnp.sin(angles)


def rope_fwd_kernel(qkv_ref, cos_ref, sin_ref, qg_ref, kg_ref, q_ref, k_ref, kt_ref, vt_ref, *, heads, head):
    half = head // 2
    cos_b, sin_b = cos_ref[...], sin_ref[...]
    for h in range(heads + 1):
        cols = slice(h * head, (h + 1) * head)
        gain = qg_ref[...] if h < heads else kg_ref[...]
        normed = rms_scale(qkv_ref[:, cols].astype(F32), gain)
        first, second = normed[:, :half], normed[:, half:]
        rotated = jnp.concatenate([first * cos_b - second * sin_b, second * cos_b + first * sin_b], axis=-1)
        if h < heads:
            q_ref[:, cols] = rotated.astype(BF16)
        else:
            k_ref[...] = rotated.astype(BF16)
            kt_ref[...] = rotated.T.astype(BF16)
    vt_ref[...] = qkv_ref[:, (heads + 1) * head:].astype(F32).T.astype(BF16)


def rope_bwd_kernel(qkv_ref, dq_ref, dk_ref, dv_ref, cos_ref, sin_ref, qg_ref, kg_ref, dqkv_ref, dqg_ref, dkg_ref, *, heads, head):
    half = head // 2
    cos_b, sin_b = cos_ref[...], sin_ref[...]

    @pl.when(pl.program_id(0) == 0)
    def _():
        dqg_ref[...] = jnp.zeros_like(dqg_ref)
        dkg_ref[...] = jnp.zeros_like(dkg_ref)

    for h in range(heads + 1):
        cols = slice(h * head, (h + 1) * head)
        gain = 1.0 + (qg_ref[...] if h < heads else kg_ref[...])
        d_rot = (dq_ref[:, cols] if h < heads else dk_ref[...]).astype(F32)
        first, second = d_rot[:, :half], d_rot[:, half:]
        d_normed = jnp.concatenate([first * cos_b + second * sin_b, second * cos_b - first * sin_b], axis=-1)
        x_f32 = qkv_ref[:, cols].astype(F32)
        inv_rms = lax.rsqrt(jnp.mean(x_f32 * x_f32, axis=-1, keepdims=True) + EPS)
        unit = x_f32 * inv_rms
        d_gain = jnp.sum(d_normed * unit, axis=0, keepdims=True)
        if h < heads:
            dqg_ref[...] += d_gain
        else:
            dkg_ref[...] += d_gain
        d_unit = d_normed * gain
        d_x = inv_rms * (d_unit - unit * jnp.mean(d_unit * unit, axis=-1, keepdims=True))
        dqkv_ref[:, cols] = d_x.astype(BF16)
    dqkv_ref[:, (heads + 1) * head:] = dv_ref[...]


def rope_specs(block, heads, head):
    tall = lambda cols: pl.BlockSpec((block, cols), lambda i: (i, 0))
    flat = pl.BlockSpec((head, block), lambda i: (0, i))
    fixed = pl.BlockSpec((1, head), lambda i: (0, 0))
    return tall, flat, fixed


def rope_fwd(qkv, cosines, sines, q_gain, k_gain, heads, head):
    seq, wide = qkv.shape
    block = min(BLOCK, seq)
    tall, flat, fixed = rope_specs(block, heads, head)
    return pl.pallas_call(
        functools.partial(rope_fwd_kernel, heads=heads, head=head),
        grid=(seq // block,),
        in_specs=[tall(wide), tall(head // 2), tall(head // 2), fixed, fixed],
        out_specs=[tall(heads * head), tall(head), flat, flat],
        out_shape=[
            jax.ShapeDtypeStruct((seq, heads * head), BF16),
            jax.ShapeDtypeStruct((seq, head), BF16),
            jax.ShapeDtypeStruct((head, seq), BF16),
            jax.ShapeDtypeStruct((head, seq), BF16),
        ],
        compiler_params=pltpu.CompilerParams(dimension_semantics=('arbitrary',), vmem_limit_bytes=40 * 2 ** 20),
        cost_estimate=pl.CostEstimate(flops=20 * seq * wide, bytes_accessed=4 * seq * wide, transcendentals=seq),
        name='rope_fwd',
    )(qkv, cosines, sines, q_gain, k_gain)


def rope_bwd(qkv, dq, dk, dv, cosines, sines, q_gain, k_gain, heads, head):
    seq, wide = qkv.shape
    block = min(BLOCK, seq)
    tall, flat, fixed = rope_specs(block, heads, head)
    return pl.pallas_call(
        functools.partial(rope_bwd_kernel, heads=heads, head=head),
        grid=(seq // block,),
        in_specs=[tall(wide), tall(heads * head), tall(head), tall(head), tall(head // 2), tall(head // 2), fixed, fixed],
        out_specs=[tall(wide), fixed, fixed],
        out_shape=[
            jax.ShapeDtypeStruct((seq, wide), BF16),
            jax.ShapeDtypeStruct((1, head), F32),
            jax.ShapeDtypeStruct((1, head), F32),
        ],
        compiler_params=pltpu.CompilerParams(dimension_semantics=('arbitrary',), vmem_limit_bytes=40 * 2 ** 20),
        cost_estimate=pl.CostEstimate(flops=30 * seq * wide, bytes_accessed=6 * seq * wide, transcendentals=seq),
        name='rope_bwd',
    )(qkv, dq, dk, dv, cosines, sines, q_gain, k_gain)


def below_diagonal(block):
    keys = lax.broadcasted_iota(jnp.int32, (block, block), 0)
    queries = lax.broadcasted_iota(jnp.int32, (block, block), 1)
    return keys <= queries


def fwd_kernel(q_ref, k_ref, vt_ref, o_ref, lse_ref, acc, top, total, *, block, head):
    index = pl.program_id(0)
    mult = LOG2E * head ** -0.5

    def step(j, first):
        start = pl.multiple_of(j * block, block)
        keys = k_ref[pl.ds(start, block), :]
        vals = vt_ref[:, pl.ds(start, block)]
        for h in range(PAIR):
            query = q_ref[:, h * head:(h + 1) * head]
            scores = lax.dot_general(keys, query, NT, preferred_element_type=F32) * mult
            if first:
                scores = jnp.where(below_diagonal(block), scores, NEG_BIG)
                peak = jnp.max(scores, axis=0, keepdims=True)
                prob = jnp.exp2(scores - peak)
                total[h] = jnp.sum(prob, axis=0, keepdims=True)
                acc[h] = jnp.dot(vals, prob.astype(BF16), preferred_element_type=F32)
            else:
                old = top[h]
                peak = jnp.maximum(old, jnp.max(scores, axis=0, keepdims=True))
                prob = jnp.exp2(scores - peak)
                fade = jnp.exp2(old - peak)
                total[h] = total[h] * fade + jnp.sum(prob, axis=0, keepdims=True)
                acc[h] = acc[h] * fade + jnp.dot(vals, prob.astype(BF16), preferred_element_type=F32)
            top[h] = peak

    step(index, True)

    @pl.loop(0, index)
    def _(j):
        step(j, False)

    for h in range(PAIR):
        out = acc[h] / total[h]
        o_ref[:, h * head:(h + 1) * head] = out.T.astype(BF16)
        lse_ref[h] = top[h] + jnp.log2(total[h])


def bwd_kernel(q_ref, do_ref, lse_ref, delta_ref, k_ref, v_ref, kt_ref, dq_ref, dk_ref, dv_ref, dk_acc, dv_acc, dqt, *, block, head):
    index = pl.program_id(0)
    pair = pl.program_id(1)
    scale = head ** -0.5
    mult = LOG2E * scale

    @pl.when((index == 0) & (pair == 0))
    def _():
        dk_acc[...] = jnp.zeros_like(dk_acc)
        dv_acc[...] = jnp.zeros_like(dv_acc)

    def step(j, first):
        start = pl.multiple_of(j * block, block)
        rows = pl.ds(start, block)
        keys = k_ref[rows, :]
        vals = v_ref[rows, :]
        keys_t = kt_ref[:, rows]
        dk_part = []
        dv_part = []
        for h in range(PAIR):
            cols = slice(h * head, (h + 1) * head)
            query = q_ref[:, cols]
            d_out = do_ref[:, cols]
            scores = lax.dot_general(keys, query, NT, preferred_element_type=F32)
            prob = jnp.exp2(scores * mult - lse_ref[h])
            if first:
                prob = jnp.where(below_diagonal(block), prob, 0.0)
            d_prob = lax.dot_general(vals, d_out, NT, preferred_element_type=F32)
            d_score = (prob * (d_prob - delta_ref[h])).astype(BF16)
            dv_part.append(jnp.dot(prob.astype(BF16), d_out, preferred_element_type=F32))
            dk_part.append(jnp.dot(d_score, query, preferred_element_type=F32))
            dq_part = jnp.dot(keys_t, d_score, preferred_element_type=F32)
            if first:
                dqt[h] = dq_part
            else:
                dqt[h] += dq_part
        dk_acc[rows, :] += sum(dk_part)
        dv_acc[rows, :] += sum(dv_part)

    step(index, True)

    @pl.loop(0, index)
    def _(j):
        step(j, False)

    for h in range(PAIR):
        dq_ref[:, h * head:(h + 1) * head] = (dqt[h].T * scale).astype(BF16)

    @pl.when((index == pl.num_programs(0) - 1) & (pair == pl.num_programs(1) - 1))
    def _():
        dk_ref[...] = (dk_acc[...] * scale).astype(BF16)
        dv_ref[...] = dv_acc[...].astype(BF16)


def attention_fwd(q, k, v_t, head):
    seq, wide = q.shape
    heads = wide // head
    block = min(BLOCK, seq)
    flops = 2 * 2 * heads * seq * (seq + block) // 2 * head
    whole = lambda *_: (0, 0)
    return pl.pallas_call(
        functools.partial(fwd_kernel, block=block, head=head),
        grid=(seq // block, heads // PAIR),
        in_specs=[
            pl.BlockSpec((block, PAIR * head), lambda i, p: (i, p)),
            pl.BlockSpec((seq, head), whole),
            pl.BlockSpec((head, seq), whole),
        ],
        out_specs=[
            pl.BlockSpec((block, PAIR * head), lambda i, p: (i, p)),
            pl.BlockSpec((PAIR, 1, block), lambda i, p: (p, 0, i)),
        ],
        out_shape=[
            jax.ShapeDtypeStruct((seq, wide), BF16),
            jax.ShapeDtypeStruct((heads, 1, seq), F32),
        ],
        scratch_shapes=[
            pltpu.VMEM((PAIR, head, block), F32),
            pltpu.VMEM((PAIR, 1, block), F32),
            pltpu.VMEM((PAIR, 1, block), F32),
        ],
        compiler_params=pltpu.CompilerParams(
            dimension_semantics=('arbitrary', 'arbitrary'), vmem_limit_bytes=48 * 2 ** 20),
        cost_estimate=pl.CostEstimate(flops=flops, bytes_accessed=4 * seq * wide, transcendentals=heads * seq * seq // 2),
        name='attn_fwd',
    )(q, k, v_t)


def attention_bwd(q, k, k_t, qkv, lse, d_out, delta, head):
    seq, wide = q.shape
    heads = wide // head
    block = min(BLOCK, seq)
    flops = 5 * 2 * heads * seq * (seq + block) // 2 * head
    whole = lambda *_: (0, 0)
    wide_spec = pl.BlockSpec((block, PAIR * head), lambda i, p: (i, p))
    row_spec = pl.BlockSpec((PAIR, 1, block), lambda i, p: (p, 0, i))
    return pl.pallas_call(
        functools.partial(bwd_kernel, block=block, head=head),
        grid=(seq // block, heads // PAIR),
        in_specs=[
            wide_spec, wide_spec, row_spec, row_spec,
            pl.BlockSpec((seq, head), whole),
            pl.BlockSpec((seq, head), lambda *_: (0, heads + 1)),
            pl.BlockSpec((head, seq), whole),
        ],
        out_specs=[wide_spec, pl.BlockSpec((seq, head), whole), pl.BlockSpec((seq, head), whole)],
        out_shape=[
            jax.ShapeDtypeStruct((seq, wide), BF16),
            jax.ShapeDtypeStruct((seq, head), BF16),
            jax.ShapeDtypeStruct((seq, head), BF16),
        ],
        scratch_shapes=[
            pltpu.VMEM((seq, head), F32),
            pltpu.VMEM((seq, head), F32),
            pltpu.VMEM((PAIR, head, block), F32),
        ],
        compiler_params=pltpu.CompilerParams(
            dimension_semantics=('arbitrary', 'arbitrary'), vmem_limit_bytes=56 * 2 ** 20),
        cost_estimate=pl.CostEstimate(flops=flops, bytes_accessed=6 * seq * wide, transcendentals=heads * seq * seq // 2),
        name='attn_bwd',
    )(q, d_out, lse, delta, k, qkv, k_t)


def matmul(a, b):
    return jnp.dot(a, b, preferred_element_type=F32)


def solution(mesh):
    group = mesh.shape['sp']

    def exchange(arr):
        return lax.all_to_all(arr, 'sp', 0, 0, tiled=True)

    def spread_sum(grad):
        part = lax.psum_scatter(grad, 'sp', scatter_dimension=0, tiled=True)
        return lax.all_gather(part.astype(BF16), 'sp', axis=0, tiled=True)

    def device_step(x_in, dy_in, positions, w_q, w_k, w_v, w_o, w_pre, w_post, q_norm, k_norm):
        batch, seq_loc, width = x_in.shape
        head = q_norm.shape[0]
        heads = w_q.shape[1] // head
        q_wide = heads * head
        seq = group * seq_loc
        rounds = batch // group
        x_seqs = [exchange(x_in[r * group:(r + 1) * group]).reshape(seq, width) for r in range(rounds)]
        dy_seqs = [exchange(dy_in[r * group:(r + 1) * group]).reshape(seq, width) for r in range(rounds)]
        pos_all = lax.all_gather(positions, 'sp', axis=0, tiled=True)
        cosines, sines = rope_tables(pos_all, head)
        gains = (q_norm[None, :], k_norm[None, :])
        w_qkv = jnp.concatenate([w_q, w_k, w_v], axis=1)
        cut = lambda arr, h: arr[:, h * head:(h + 1) * head]

        y_parts, saved = [], []
        dw_o = dw_post = 0.0
        for r in range(rounds):
            x_f32 = x_seqs[r].astype(F32)
            normed, pre_pull = jax.vjp(pre_norm, x_f32, w_pre)
            qkv = matmul(normed, w_qkv).astype(BF16)
            q_rot, k_rot, k_t, v_t = rope_fwd(qkv, cosines, sines, *gains, heads, head)
            o_flat, lse = attention_fwd(q_rot, k_rot, v_t, head)
            proj = matmul(o_flat, w_o).astype(BF16)
            post, post_pull = jax.vjp(post_norm, proj, w_post)
            y_parts.append(exchange((x_f32 + post).astype(BF16).reshape(group, seq_loc, width)))
            dy_f32 = dy_seqs[r].astype(F32)
            d_proj, dw_post_r = post_pull(dy_f32)
            dw_post += dw_post_r
            dw_o += lax.dot_general(o_flat, d_proj, (((0,), (0,)), ((), ())), preferred_element_type=F32)
            d_oflat = lax.dot_general(d_proj, w_o, NT, preferred_element_type=F32).astype(BF16)
            delta = jnp.stack([jnp.sum(cut(d_oflat, h).astype(F32) * cut(o_flat, h).astype(F32), axis=-1) for h in range(heads)])[:, None, :]
            saved.append((normed, pre_pull, qkv, q_rot, k_rot, k_t, lse, d_oflat, delta, dy_f32))
        dw_o = spread_sum(dw_o)

        dx_parts = []
        dw_qkv = dw_pre = dq_norm = dk_norm = 0.0
        for r in range(rounds):
            normed, pre_pull, qkv, q_rot, k_rot, k_t, lse, d_oflat, delta, dy_f32 = saved[r]
            dq_rot, dk_rot, dv_proj = attention_bwd(q_rot, k_rot, k_t, qkv, lse, d_oflat, delta, head)
            d_qkv, d_qg, d_kg = rope_bwd(qkv, dq_rot, dk_rot, dv_proj, cosines, sines, *gains, heads, head)
            dq_norm += d_qg[0]
            dk_norm += d_kg[0]
            d_normed = lax.dot_general(d_qkv, w_qkv, NT, preferred_element_type=F32).astype(BF16)
            dx_norm, dw_pre_r = pre_pull(d_normed)
            dw_pre += dw_pre_r
            dx_parts.append(exchange((dy_f32 + dx_norm).astype(BF16).reshape(group, seq_loc, width)))
            dw_qkv += lax.dot_general(normed, d_qkv, (((0,), (0,)), ((), ())), preferred_element_type=F32)
        dw_qkv = spread_sum(dw_qkv)
        kv_wide = w_k.shape[1]
        sums = lax.psum((dw_pre, dw_post, dq_norm, dk_norm), 'sp')
        return (jnp.concatenate(y_parts, axis=0), jnp.concatenate(dx_parts, axis=0),
                dw_qkv[:, :q_wide], dw_qkv[:, q_wide:q_wide + kv_wide], dw_qkv[:, q_wide + kv_wide:], dw_o) + sums

    token_spec = P('dp', 'sp', None)
    return jax.shard_map(device_step, mesh=mesh,
                         in_specs=(token_spec, token_spec, P(('dp', 'sp')), P(None, None), P(None, None), P(None, None), P(None, None), P(None), P(None), P(None), P(None)),
                         out_specs=(token_spec, token_spec, P('dp', None), P('dp', None), P('dp', None), P('dp', None), P('dp'), P('dp'), P('dp'), P('dp')),
                         check_vma=False)
```

time: 3360 us -> 1580 us (0.47)
  matrix products: 1160 us -> 240 us
  waiting for transfers between devices: 820 us -> 146 us
  Pallas kernels: 0 us -> 531 us
  other arithmetic: 668 us -> 168 us
  local copies, waits for them, and re-layouts: 424 us -> 55.3 us
  blocking collectives: 203 us -> 383 us
    dot_general x36 -> x12, matrix products: 1160 us -> 240 us  [the longest x4 87 us: matmul(): return jnp.dot(a, b, preferred_element_type=F32)]
    all_to_all x8 -> x7, waiting for transfers between devices: 820 us -> 146 us  [exchange(): return lax.all_to_all(arr, 'sp', 0, 0, tiled=True)]
    pallas_call x0 -> x8, Pallas kernels: none -> 531 us  [the longest x2 266 us: attention_bwd(): pl.pallas_call(functools.partial(bwd_kernel, block=block, head=head), gri...]
    another operation x5 -> x2, other arithmetic: 277 us -> 0.14 us  [device_step(): jnp.stack([jnp.sum(cut(d_oflat, h).astype(F32) * cut(o_flat, h).astype(F3...]
    all_to_all x0 -> x1, blocking collectives: none -> 150 us  [exchange(): return lax.all_to_all(arr, 'sp', 0, 0, tiled=True)]
    all_to_all x7 -> x0, local copies, waits for them, and re-layouts: 126 us -> none  [the longest x5 93.7 us: to_heads(): return lax.all_to_all(arr, 'sp', 2, 1, tiled=True)]
    reduce_sum x6 -> x2, other arithmetic: 130 us -> 14.7 us  [device_step(): jnp.sum(cut(d_oflat, h).astype(F32) * cut(o_flat, h).astype(F32), axis=-1)]
    all_gather x0 -> x1, blocking collectives: none -> 106 us  [device_step(): pos_all = lax.all_gather(positions, 'sp', axis=0, tiled=True)]
  transfers between devices with their start and end apart: 8 -> 11, of which waited for: 7 -> 2; matrix products, arithmetic and copies ran while one was open for 27% -> 27% of each run, Pallas kernels for 0% -> 34%
where the time goes in v1:
time: 1580 us
  Pallas kernels  531 us (34%)
  blocking collectives  383 us (24%)
  matrix products  240 us (15%)
  other arithmetic  168 us (11%)
  waiting for transfers between devices  146 us (9%)
  local copies, waits for them, and re-layouts  55.3 us (4%)
  starting transfers between devices  42.1 us (3%)
    pallas_call x2, Pallas kernels, attention_bwd(): pl.pallas_call(functools.partial(bwd_kernel, block=block, head=head), gri...  266 us
    pallas_call x2, Pallas kernels, attention_fwd(): pl.pallas_call(functools.partial(fwd_kernel, block=block, head=head), gri...  203 us
    all_to_all x1, blocking collectives, exchange(): return lax.all_to_all(arr, 'sp', 0, 0, tiled=True)  150 us
    all_to_all x7, waiting for transfers between devices, exchange(): return lax.all_to_all(arr, 'sp', 0, 0, tiled=True)  146 us
    psum x1, blocking collectives, device_step(): sums = lax.psum((dw_pre, dw_post, dq_norm, dk_norm), 'sp')  127 us
    all_gather x1, blocking collectives, device_step(): pos_all = lax.all_gather(positions, 'sp', axis=0, tiled=True)  106 us
    dot_general x4, matrix products, matmul(): return jnp.dot(a, b, preferred_element_type=F32)  87 us
    dot_general x2, matrix products, device_step(): lax.dot_general(d_qkv, w_qkv, NT, preferred_element_type=F32).astype(BF16)  53.8 us
  transfers between devices with their start and end apart: 11, of which 2 were waited for; matrix products, arithmetic and copies ran while one was open for 27% of the time, Pallas kernels for 34%

profile of v1, /device:TPU:0, one launch (start us, length us, event | category | flops | bytes accessed | tf_op | source)
XLA Modules:
  0.0 1581.3 jit_solution(3444368836471878900)
XLA Ops:
  27.9 106.4 %all_gather.9 = s32[4096]{0:T(1024)S(1)} all-gather(s32[1024]{0:T(1024)S(1)} %copy-done.46), channel_id=1, replica_groups=mesh['dp'=2,'sp'=4] {'sp'}, dimensions={0}, use_global_device_ids=true | all-gather | bytes 20480 | tf_op jit(solution)/shard_map/all_gather | solution.py:325
  185.1 72.7 %all-to-all-done.2 = bf16[4,1024,1152]{2,1,0:T(8,128)(2,1)} async-done(((bf16[4,1024,1152]{2,1,0:T(8,128)(2,1)}), bf16[4,1024,1152]{2,1,0:T(8,128)(2,1)}, u32[]{:S(2)}, u32[]{:S(2)}) %all-to-all-start.2) | async-done | bytes 9437216 | tf_op jit(solution)/shard_map/all_to_all | solution.py:310
  264.0 23.1 %convolution_convert_fusion.5.qkv_ref.v_ref = bf16[4096,1536]{1,0:T(8,128)(2,1)} fusion(bf16[4096,1152]{1,0:T(8,128)(2,1)} %fusion.30, bf16[1152,1536]{1,0:T(8,128)(2,1)} %constant_dynamic-update-slice_fusion), kind=kOutput, calls=%fused_computation.67 | convolution fusion | flops 14501806080 | bytes 25559040 | tf_op jit(solution)/shard_map/dot_general | solution.py:303
  308.3 101.1 %attn_fwd.2 = (bf16[4096,1024]{1,0:T(8,128)(2,1)}, f32[4,1,4096]{2,1,0:T(1,128)S(1)}) custom-call(bf16[4096,1024]{1,0:T(8,128)(2,1)} %get-tuple-element.34.q_ref, bf16[4096,256]{1,0:T(8,128)(2,1)S(1)} %get-tuple-element.35.k_ref, bf16[256,4096]{1,0:T(8,128)(2,1)S(1)} %get-tuple-element.36.vt_ref), custom_call_target="tpu_custom_call" | custom-call | flops 38654705664 | bytes 16777216 | tf_op jit(solution)/shard_map/attn_fwd/pallas_call | solution.py:239
  409.5 16.2 %fusion.22 = (f32[4096]{0:T(1024)S(1)}, bf16[4096,1152]{1,0:T(8,128)(2,1)}) fusion(bf16[4096,1024]{1,0:T(8,128)(2,1)} %get-tuple-element.37, bf16[1024,1152]{1,0:T(8,128)(2,1)S(1)} %copy-done), kind=kOutput, calls=%fused_computation.44 | convolution fusion | flops 9682546688 | bytes 20201472 | tf_op jit(solution)/shard_map/dot_general | solution.py:303
  479.0 133.3 %attn_bwd.2 = (bf16[4096,1024]{1,0:T(8,128)(2,1)}, bf16[4096,256]{1,0:T(8,128)(2,1)}, bf16[4096,256]{1,0:T(8,128)(2,1)}) custom-call(bf16[4096,1024]{1,0:T(8,128)(2,1)} %get-tuple-element.34.q_ref, bf16[4096,1024]{1,0:T(8,128)(2,1)} %convolution_convert_fusion.7.do_ref, f32[4,1,4096]{2,1,0:T(1,128)} %copy-done.22, f32[4,1,4096]{2,1,0:T(1,128)} %broadcast_in_dim.37.delta_ref, ...), custom_call_target="tpu_custom_call" | custom-call | flops 96636764160 | bytes 25165824 | tf_op jit(solution)/shard_map/attn_bwd/pallas_call | solution.py:275
  615.5 18.0 %rope_bwd.2 = (bf16[4096,1536]{1,0:T(8,128)(2,1)}, f32[1,256]{1,0:T(1,128)S(1)}, f32[1,256]{1,0:T(1,128)S(1)}) custom-call(bf16[4096,1536]{1,0:T(8,128)(2,1)} %convolution_convert_fusion.5.qkv_ref.v_ref, bf16[4096,1024]{1,0:T(8,128)(2,1)} %get-tuple-element.44.dq_ref, bf16[4096,256]{1,0:T(8,128)(2,1)S(1)} %copy-done.11, bf16[4096,256]{1,0:T(8,128)(2,1)S(1)} %copy-done.12, ...), custom_call_target="tpu_custom_call" | custom-call | flops 188743680 | bytes 37748736 | tf_op jit(solution)/shard_map/rope_bwd/pallas_call | solution.py:119
  633.6 27.2 %fusion.14 = (f32[1152]{0:T(1024)}, f32[4096]{0:T(1024)S(1)}, bf16[4096,1152]{1,0:T(8,128)(2,1)}) fusion(bf16[4,1024,1152]{2,1,0:T(8,128)(2,1)} %all-to-all-done, f32[4096]{0:T(1024)S(1)} %copy-done.37, f32[1152]{0:T(1024)S(1)} %copy-done.39, bf16[4096,1536]{1,0:T(8,128)(2,1)} %get-tuple-element.47, bf16[1152,1536]{1,0:T(8,128)(2,1)} %constant_dynamic-update-slice_fusion), kind=kOutput, calls=%fused_computation.36 | convolution fusion | flops 14537976832 | bytes 35038208 | tf_op jit(solution)/shard_map/dot_general | solution.py:359
  660.9 17.4 %fusion.18 = (bf16[4096,1152]{1,0:T(8,128)(2,1)}, bf16[4096,1152]{1,0:T(8,128)(2,1)S(1)}) fusion(bf16[4096,1152]{1,0:T(8,128)(2,1)} %get-tuple-element.94, bf16[4,1024,1152]{2,1,0:T(8,128)(2,1)} %all-to-all-done, bf16[4,1024,1152]{2,1,0:T(8,128)(2,1)} %all-to-all-done.4, f32[4096]{0:T(1024)S(1)} %fusion.37, f32[1152]{0:T(1024)S(1)} %copy-done.39, ...), kind=kLoop, calls=%fused_computation.40 | loop fusion | flops 66060288 | bytes 56676864 | tf_op jit(solution)/shard_map/convert_element_type | solution.py:362
  681.9 31.9 %convolution_convert_fusion.3.qkv_ref.v_ref = bf16[4096,1536]{1,0:T(8,128)(2,1)} fusion(bf16[4096,1152]{1,0:T(8,128)(2,1)S(1)} %get-tuple-element.91, bf16[1152,1536]{1,0:T(8,128)(2,1)} %constant_dynamic-update-slice_fusion), kind=kOutput, calls=%fused_computation.65 | convolution fusion | flops 14501806080 | bytes 25559040 | tf_op jit(solution)/shard_map/dot_general | solution.py:303
  728.2 102.0 %attn_fwd.3 = (bf16[4096,1024]{1,0:T(8,128)(2,1)}, f32[4,1,4096]{2,1,0:T(1,128)S(1)}) custom-call(bf16[4096,1024]{1,0:T(8,128)(2,1)} %get-tuple-element.38.q_ref, bf16[4096,256]{1,0:T(8,128)(2,1)S(1)} %get-tuple-element.39.k_ref, bf16[256,4096]{1,0:T(8,128)(2,1)S(1)} %get-tuple-element.40.vt_ref), custom_call_target="tpu_custom_call" | custom-call | flops 38654705664 | bytes 16777216 | tf_op jit(solution)/shard_map/attn_fwd/pallas_call | solution.py:239
  830.2 15.7 fusion.24
  845.9 16.6 %fusion.44 = f32[1024,1152]{1,0:T(8,128)} fusion(bf16[4096,1024]{1,0:T(8,128)(2,1)S(1)} %bitcast.117, bf16[4096,1152]{1,0:T(8,128)(2,1)} %copy-done.25), kind=kOutput, calls=%fused_computation.113 | convolution fusion | flops 9663676416 | bytes 22544384 | tf_op jit(solution)/shard_map/dot_general | solution.py:345
  880.1 15.7 fusion.17
  932.4 133.0 %attn_bwd.3 = (bf16[4096,1024]{1,0:T(8,128)(2,1)}, bf16[4096,256]{1,0:T(8,128)(2,1)}, bf16[4096,256]{1,0:T(8,128)(2,1)}) custom-call(bf16[4096,1024]{1,0:T(8,128)(2,1)} %get-tuple-element.38.q_ref, bf16[4096,1024]{1,0:T(8,128)(2,1)} %convolution_convert_fusion.6.do_ref, f32[4,1,4096]{2,1,0:T(1,128)} %copy-done.21, f32[4,1,4096]{2,1,0:T(1,128)} %broadcast_in_dim.40.delta_ref, ...), custom_call_target="tpu_custom_call" | custom-call | flops 96636764160 | bytes 25165824 | tf_op jit(solution)/shard_map/attn_bwd/pallas_call | solution.py:275
  1065.4 19.0 %fusion.43 = f32[1152,1536]{1,0:T(8,128)S(1)} fusion(bf16[4096,1152]{1,0:T(8,128)(2,1)} %fusion.30, bf16[4096,1536]{1,0:T(8,128)(2,1)} %get-tuple-element.47), kind=kOutput, calls=%fused_computation.112 | convolution fusion | flops 14495514624 | bytes 29097984 | tf_op jit(solution)/shard_map/dot_general | solution.py:363
  1084.5 18.0 %rope_bwd.3 = (bf16[4096,1536]{1,0:T(8,128)(2,1)}, f32[1,256]{1,0:T(1,128)S(1)}, f32[1,256]{1,0:T(1,128)S(1)}) custom-call(bf16[4096,1536]{1,0:T(8,128)(2,1)} %convolution_convert_fusion.3.qkv_ref.v_ref, bf16[4096,1024]{1,0:T(8,128)(2,1)} %get-tuple-element.50.dq_ref, bf16[4096,256]{1,0:T(8,128)(2,1)S(1)} %copy-done.9, bf16[4096,256]{1,0:T(8,128)(2,1)S(1)} %copy-done.10, ...), custom_call_target="tpu_custom_call" | custom-call | flops 188743680 | bytes 37748736 | tf_op jit(solution)/shard_map/rope_bwd/pallas_call | solution.py:119
  1102.5 21.9 %convolution_add_fusion = f32[1152,1536]{1,0:T(8,128)} fusion(f32[1152,1536]{1,0:T(8,128)S(1)} %fusion.43, bf16[4096,1152]{1,0:T(8,128)(2,1)} %copy-done.24, bf16[4096,1536]{1,0:T(8,128)(2,1)} %get-tuple-element.53), kind=kOutput, calls=%fused_computation.68 | convolution fusion | flops 14497284096 | bytes 36175872 | tf_op jit(solution)/shard_map/dot_general | solution.py:363
  1124.4 149.9 %all_to_all.40 = bf16[4,1024,1152]{2,1,0:T(8,128)(2,1)} all-to-all(bf16[4,1024,1152]{2,1,0:T(8,128)(2,1)} %bitcast.113), channel_id=1, replica_groups=mesh['dp'=2,'sp'=4] {'sp'}, dimensions={0} | all-to-all | bytes 18874368 | tf_op jit(solution)/shard_map/all_to_all | solution.py:310
  1280.4 26.5 %fusion.15 = (f32[1152]{0:T(1024)S(1)}, f32[4096]{0:T(1024)S(1)}, bf16[4096,1152]{1,0:T(8,128)(2,1)}) fusion(bf16[4,1024,1152]{2,1,0:T(8,128)(2,1)} %all-to-all-done.2, f32[4096]{0:T(1024)S(1)} %copy-done.35, f32[1152]{0:T(1024)S(1)} %copy-done.40, bf16[4096,1536]{1,0:T(8,128)(2,1)} %get-tuple-element.53, ...), kind=kOutput, calls=%fused_computation.37 | convolution fusion | flops 14537976832 | bytes 35038208 | tf_op jit(solution)/shard_map/dot_general | solution.py:359
  1323.6 73.4 %all-to-all-done.3 = bf16[4,1024,1152]{2,1,0:T(8,128)(2,1)} async-done(((bf16[4,1024,1152]{2,1,0:T(8,128)(2,1)}), bf16[4,1024,1152]{2,1,0:T(8,128)(2,1)}, u32[]{:S(2)}, u32[]{:S(2)}) %all-to-all-start.3) | async-done | bytes 9437216 | tf_op jit(solution)/shard_map/all_to_all | solution.py:310
  1405.7 127.0 %all-reduce = (f32[1152]{0:T(1024)}, f32[1152]{0:T(1024)}, f32[256]{0:T(256)}, f32[256]{0:T(256)}) all-reduce(f32[1152]{0:T(1024)S(1)} %add.116, f32[1152]{0:T(1024)S(1)} %add.117, f32[256]{0:T(256)S(1)} %bitcast.128, f32[256]{0:T(256)S(1)} %bitcast.129), channel_id=1, replica_groups=mesh['dp'=2,'sp'=4] {'sp'}, use_global_device_ids=true, to_apply=%region_20.0 | all-reduce | flops 2816 | bytes 22528 | tf_op jit(solution)/shard_map/psum | solution.py:366
  1532.6 16.5 %pad_maximum_fusion = bf16[8,1024,1152]{2,1,0:T(8,128)(2,1)} fusion(bf16[4,1024,1152]{2,1,0:T(8,128)(2,1)} %all-to-all-done.3, bf16[4,1024,1152]{2,1,0:T(8,128)(2,1)} %all-to-all-done.1), kind=kLoop, calls=%fused_computation.48 | loop fusion | flops 9437184 | bytes 37748736 | tf_op jit(solution)/shard_map/concatenate | solution.py:367
  1549.2 16.5 %pad_maximum_fusion.1 = bf16[8,1024,1152]{2,1,0:T(8,128)(2,1)} fusion(bf16[4,1024,1152]{2,1,0:T(8,128)(2,1)} %all-to-all-done.7, bf16[4,1024,1152]{2,1,0:T(8,128)(2,1)} %all_to_all.40), kind=kLoop, calls=%fused_computation.49 | loop fusion | flops 9437184 | bytes 37748736 | tf_op jit(solution)/shard_map/concatenate | solution.py:367
  (175 shorter events, 267.3 us)
Async XLA Ops:
  7.2 402.3 %copy-start = (bf16[1024,1152]{1,0:T(8,128)(2,1)S(1)}, bf16[1024,1152]{1,0:T(8,128)(2,1)}, u32[]{:S(2)}) copy-start(bf16[1024,1152]{1,0:T(8,128)(2,1)} %param.17) | copy-start | bytes 7077892
  21.9 115.7 %copy-start.26 = (bf16[1152,256]{1,0:T(8,128)(2,1)S(1)}, bf16[1152,256]{1,0:T(8,128)(2,1)}, u32[]{:S(2)}) copy-start(bf16[1152,256]{1,0:T(8,128)(2,1)} %param.15) | copy-start | bytes 1769476
  21.9 125.9 %all-to-all-start = ((bf16[4,1024,1152]{2,1,0:T(8,128)(2,1)}), bf16[4,1024,1152]{2,1,0:T(8,128)(2,1)}, u32[]{:S(2)}, u32[]{:S(2)}) async-start(bf16[4,1024,1152]{2,1,0:T(8,128)(2,1)} %get-tuple-element.80), calls=%async_computation | async-start | bytes 18874368 | tf_op jit(solution)/shard_map/all_to_all | solution.py:310
  147.8 110.0 %all-to-all-start.2 = ((bf16[4,1024,1152]{2,1,0:T(8,128)(2,1)}), bf16[4,1024,1152]{2,1,0:T(8,128)(2,1)}, u32[]{:S(2)}, u32[]{:S(2)}) async-start(bf16[4,1024,1152]{2,1,0:T(8,128)(2,1)} %get-tuple-element.81), calls=%async_computation.2 | async-start | bytes 18874368 | tf_op jit(solution)/shard_map/all_to_all | solution.py:310
  153.8 289.6 %copy-start.28 = (f32[1152]{0:T(1024)}, f32[1152]{0:T(1024)S(1)}, u32[]{:S(2)}) copy-start(f32[1152]{0:T(1024)S(1)} %broadcast_add_fusion) | copy-start | bytes 13828
  257.8 167.9 %all-to-all-start.4 = ((bf16[4,1024,1152]{2,1,0:T(8,128)(2,1)}), bf16[4,1024,1152]{2,1,0:T(8,128)(2,1)}, u32[]{:S(2)}, u32[]{:S(2)}) async-start(bf16[4,1024,1152]{2,1,0:T(8,128)(2,1)} %get-tuple-element.78), calls=%async_computation.4 | async-start | bytes 18874368 | tf_op jit(solution)/shard_map/all_to_all | solution.py:310
  301.4 108.1 %copy-start.19 = (bf16[4096,256]{1,0:T(8,128)(2,1)}, bf16[4096,256]{1,0:T(8,128)(2,1)S(1)}, u32[]{:S(2)}) copy-start(bf16[4096,256]{1,0:T(8,128)(2,1)S(1)} %get-tuple-element.35.k_ref) | copy-start | bytes 6291460
  307.7 101.8 %copy-start.30 = (f32[1,8,4,128]{3,2,1,0:T(4,128)}, f32[1,8,4,128]{3,2,1,0:T(4,128)S(1)}, u32[]{:S(2)}) copy-start(f32[1,8,4,128]{3,2,1,0:T(4,128)S(1)} %add_bitcast_fusion) | copy-start | bytes 49156
  425.7 436.8 %all-to-all-start.6 = ((bf16[4,1024,1152]{2,1,0:T(8,128)(2,1)}), bf16[4,1024,1152]{2,1,0:T(8,128)(2,1)}, u32[]{:S(2)}, u32[]{:S(2)}) async-start(bf16[4,1024,1152]{2,1,0:T(8,128)(2,1)} %get-tuple-element.79), calls=%async_computation.6 | async-start | bytes 18874368 | tf_op jit(solution)/shard_map/all_to_all | solution.py:310
  479.0 133.4 %copy-start.2 = (f32[4096,128]{1,0:T(8,128)S(1)}, f32[4096,128]{1,0:T(8,128)}, u32[]{:S(2)}) copy-start(f32[4096,128]{1,0:T(8,128)} %get-tuple-element.88.sin_ref) | copy-start | bytes 6291460
  479.0 133.4 %copy-start.6 = (f32[4096,128]{1,0:T(8,128)S(1)}, f32[4096,128]{1,0:T(8,128)}, u32[]{:S(2)}) copy-start(f32[4096,128]{1,0:T(8,128)} %get-tuple-element.89.cos_ref) | copy-start | bytes 6291460
  479.0 133.4 %copy-start.14 = (f32[256]{0:T(256)S(1)}, f32[256]{0:T(256)}, u32[]{:S(2)}) copy-start(f32[256]{0:T(256)} %param.20) | copy-start | bytes 3076
  479.0 133.4 %copy-start.16 = (f32[256]{0:T(256)S(1)}, f32[256]{0:T(256)}, u32[]{:S(2)}) copy-start(f32[256]{0:T(256)} %param.21) | copy-start | bytes 3076
  681.9 31.9 %copy-start.7 = (f32[4096,128]{1,0:T(8,128)S(1)}, f32[4096,128]{1,0:T(8,128)}, u32[]{:S(2)}) copy-start(f32[4096,128]{1,0:T(8,128)} %get-tuple-element.89.cos_ref) | copy-start | bytes 6291460
  713.8 132.1 %slice-start = ((s8[8388608]{0:T(1024)(128)(4,1)}), s8[4194304]{0:T(1024)(128)(4,1)S(1)}, s32[]{:S(2)}) async-start(s8[8388608]{0:T(1024)(128)(4,1)} %bitcast.116), calls=%async_computation.14 | async-start | bytes 8388608
  728.2 102.0 %copy-start.17 = (bf16[4096,256]{1,0:T(8,128)(2,1)}, bf16[4096,256]{1,0:T(8,128)(2,1)S(1)}, u32[]{:S(2)}) copy-start(bf16[4096,256]{1,0:T(8,128)(2,1)S(1)} %get-tuple-element.39.k_ref) | copy-start | bytes 6291460
  728.2 117.7 %slice-start.1 = ((s8[8388608]{0:T(1024)(128)(4,1)}), s8[4194304]{0:T(1024)(128)(4,1)S(1)}, s32[]{:S(2)}) async-start(s8[8388608]{0:T(1024)(128)(4,1)} %bitcast.116), calls=%async_computation.15 | async-start | bytes 8388608
  862.5 261.9 %all-to-all-start.1 = ((bf16[4,1024,1152]{2,1,0:T(8,128)(2,1)}), bf16[4,1024,1152]{2,1,0:T(8,128)(2,1)}, u32[]{:S(2)}, u32[]{:S(2)}) async-start(bf16[4,1024,1152]{2,1,0:T(8,128)(2,1)} %bitcast.112), calls=%async_computation.1 | async-start | bytes 18874368 | tf_op jit(solution)/shard_map/all_to_all | solution.py:310
  868.5 438.6 %reduce-scatter.5.cloned.1.call-start = ((), (), s32[]{:S(2)}) async-start(), calls=%async_computation.12 | async-start | bytes 5898240 | tf_op jit(solution)/shard_map/reduce_scatter | solution.py:313
  932.3 470.7 %reduce-scatter.3.cloned.1.call-start = ((), (), s32[]{:S(2)}) async-start(), calls=%async_computation.10 | async-start | bytes 8847360 | tf_op jit(solution)/shard_map/reduce_scatter | solution.py:313
  1274.3 122.7 %all-to-all-start.3 = ((bf16[4,1024,1152]{2,1,0:T(8,128)(2,1)}), bf16[4,1024,1152]{2,1,0:T(8,128)(2,1)}, u32[]{:S(2)}, u32[]{:S(2)}) async-start(bf16[4,1024,1152]{2,1,0:T(8,128)(2,1)} %bitcast.114), calls=%async_computation.3 | async-start | bytes 18874368 | tf_op jit(solution)/shard_map/all_to_all | solution.py:310
  1280.4 285.3 %all-gather.5.cloned.1.call-start = ((), (), s32[]{:S(2)}) async-start(), calls=%async_computation.13 | async-start | bytes 2949120 | tf_op jit(solution)/shard_map/all_gather | solution.py:314
  1397.1 152.1 %all-to-all-start.7 = ((bf16[4,1024,1152]{2,1,0:T(8,128)(2,1)}), bf16[4,1024,1152]{2,1,0:T(8,128)(2,1)}, u32[]{:S(2)}, u32[]{:S(2)}) async-start(bf16[4,1024,1152]{2,1,0:T(8,128)(2,1)} %bitcast.115), calls=%async_computation.7 | async-start | bytes 18874368 | tf_op jit(solution)/shard_map/all_to_all | solution.py:310
  1403.0 162.7 %all-gather.3.cloned.1.call-start = ((), (), s32[]{:S(2)}) async-start(), calls=%async_computation.11 | async-start | bytes 4423680 | tf_op jit(solution)/shard_map/all_gather | solution.py:314
  (38 other events, 527.1 us)
Sparse Core Ops, SparseCore 0:
  932.4 66.8 reduce-scatter.4
  1124.5 98.1 reduce-scatter.2
  1309.3 37.0 all-gather.4
  1405.7 50.1 all-gather.2
